TPU v7x, 32 devices: a whole 2x2x4 slice. The times are simulated.
32 devices in a mesh: gx: 4 (over x, core), gy: 2 (over y), gz: 4 (over z).
Axes of the slice: x: 2, y: 2, z: 4, core: 2. Of those that a mesh axis runs over, the one named last changes fastest.
Arguments:
- query: bfloat16 [8, 32, 128], replicated, may hold values from -12 to 12
- k_cache: bfloat16 [8, 8192, 8, 128], P(None, ('gx', 'gy', 'gz')), may hold values from -6 to 6
- v_cache: bfloat16 [8, 8192, 8, 128], P(None, ('gx', 'gy', 'gz')), may hold values from -6 to 6
- head_gain: float32 [32, 128], replicated, may hold values from 0.5 to 1.5
Outputs:
- attended: float32 [8, 32, 128], replicated
- log_norm: float32 [8, 32], replicated
- max_logit: float32 [8, 32], replicated
All inputs are finite; a program needn't handle non-finite values.
Results may differ from a plain program's by a relative error of at most 0.0003.
Values sent between devices are 32-bit elements.
A program may use at most 64 MiB of HBM per device.

v0:
```python
import jax
import jax.numpy as jnp
from jax import lax
from jax.sharding import PartitionSpec as P


def combined_all(part, axis, combine):
    gathered = jax.tree.map(lambda a: lax.all_gather(a, axis), part)

    def take(source):
        return jax.tree.map(lambda a: lax.dynamic_index_in_dim(a, source, 0, False), gathered)

    return lax.fori_loop(
        1, lax.axis_size(axis), lambda source, state: combine(state, take(source)), take(0)
    )


def finish(summed, total, highest, gain_rows):
    mixed = summed / total[..., None]
    spread_sq = jnp.mean(mixed * mixed, axis=-1, keepdims=True)
    return (mixed * lax.rsqrt(spread_sq + 1e-06) * gain_rows, highest + jnp.log(total))


def pair_fold(first_part, second_part):
    peak_one, total_one, summed_one = first_part
    peak_two, total_two, summed_two = second_part
    highest = jnp.maximum(peak_one, peak_two)
    scale_one = jnp.exp(peak_one - highest)
    scale_two = jnp.exp(peak_two - highest)
    total = total_one * scale_one + total_two * scale_two
    summed = summed_one * scale_one[..., None] + summed_two * scale_two[..., None]
    return (highest, total, summed)


def on_device(query, k_cache, v_cache, head_gain):
    batch_count, head_count, head_size = query.shape
    kv_count = k_cache.shape[2]
    group_size = head_count // kv_count
    scaling = head_size ** (-0.5)
    grouped = query.reshape(batch_count, kv_count, group_size, head_size)
    scores = (
        jnp.einsum("bkgd,btkd->bkgt", grouped, k_cache, preferred_element_type=jnp.float32)
        * scaling
    )
    local_peak = jnp.max(scores, axis=-1)
    weights = jnp.exp(scores - local_peak[..., None])
    local_total = jnp.sum(weights, axis=-1).reshape(batch_count, head_count)
    local_summed = jnp.einsum(
        "bkgt,btkd->bkgd",
        weights,
        v_cache,
        preferred_element_type=jnp.float32,
        precision=lax.Precision.HIGHEST,
    ).reshape(batch_count, head_count, head_size)
    local_peak = local_peak.reshape(batch_count, head_count)
    partial_value = combined_all((local_peak, local_total, local_summed), "gz", pair_fold)
    partial_value = combined_all(partial_value, "gy", pair_fold)
    highest, total, summed = combined_all(partial_value, "gx", pair_fold)
    attended, log_norm = finish(summed, total, highest, head_gain[None, :, :])
    return (attended, log_norm, highest)


def solution(mesh):
    in_specs = (
        P(),
        P(None, ("gx", "gy", "gz"), None, None),
        P(None, ("gx", "gy", "gz"), None, None),
        P(),
    )
    out_specs = (P(), P(), P())
    return jax.shard_map(
        on_device, mesh=mesh, in_specs=in_specs, out_specs=out_specs, check_vma=False
    )
```

profile of v0, /device:TPU:0, one launch (start us, length us, event | category | flops | bytes accessed | tf_op | source)
XLA Modules:
  0.0 88.5 jit_solution(3486891716040488848)
XLA Ops:
  0.6 0.8 copy-done
  1.5 3.4 %fusion.27 = (f32[8,8,4]{2,1,0:T(8,128)S(1)}, f32[8,8,4,256]{3,2,1,0:T(4,128)S(1)}) fusion(bf16[8,8,4,128]{3,2,1,0:T(4,128)(2,1)S(1)} %bitcast.95, bf16[8,256,8,128]{3,2,1,0:T(8,128)(2,1)} %param.9), kind=kOutput, calls=%fused_computation.54 | convolution fusion | flops 16908032 | bytes 4523008 | tf_op jit(solution)/shard_map/bkgd,btkd->bkgt/dot_general | solution.py:42
  5.1 14.8 %all_gather.39 = f32[4,8,32]{2,1,0:T(8,128)S(1)} all-gather(f32[1,8,32]{2,1,0:T(8,128)S(1)} %copy.18), channel_id=1, replica_groups=mesh['gx'=4,'gy'=2,'gz'=4] {'gz'}, dimensions={0}, use_global_device_ids=true | all-gather | bytes 5120 | tf_op jit(solution)/shard_map/all_gather | solution.py:8
  19.9 0.3 fusion.13
  20.2 4.0 %fusion.6 = f32[8,8,4,128]{3,2,1,0:T(4,128)S(1)} fusion(bf16[8,256,8,128]{3,2,1,0:T(8,128)(2,1)} %param.10, f32[8,8,4,256]{3,2,1,0:T(4,128)S(1)} %get-tuple-element.437, f32[8,8,4]{2,1,0:T(8,128)S(1)} %get-tuple-element.436), kind=kOutput, calls=%fused_computation.16 | convolution fusion | flops 100728832 | bytes 4588544 | tf_op jit(solution)/shard_map/bkgt,btkd->bkgd/dot_general | solution.py:48
  24.4 13.1 %all_gather.40 = f32[4,8,32]{2,1,0:T(8,128)S(1)} all-gather(f32[1,8,32]{2,1,0:T(8,128)S(1)} %copy.20), channel_id=1, replica_groups=mesh['gx'=4,'gy'=2,'gz'=4] {'gz'}, dimensions={0}, use_global_device_ids=true | all-gather | bytes 5120 | tf_op jit(solution)/shard_map/all_gather | solution.py:8
  37.6 15.2 %all_gather.41 = f32[4,8,32,128]{3,2,1,0:T(8,128)S(1)} all-gather(f32[1,8,32,128]{3,2,1,0:T(8,128)S(1)} %bitcast.96), channel_id=1, replica_groups=mesh['gx'=4,'gy'=2,'gz'=4] {'gz'}, dimensions={0}, use_global_device_ids=true | all-gather | bytes 655360 | tf_op jit(solution)/shard_map/all_gather | solution.py:8
  52.8 0.6 while.45
  52.9 0.2 fusion.34
  53.1 0.2 fusion.34
  53.3 0.2 fusion.34
  53.5 4.3 %all-gather = f32[16,32]{1,0:T(8,128)S(1)} all-gather(f32[8,32]{1,0:T(8,128)S(1)} %get-tuple-element.383), channel_id=2, replica_groups=mesh['gx'=4,'gy'=2,'gz'=4] {'gy'}, dimensions={0}, use_global_device_ids=true | all-gather | bytes 3072 | tf_op jit(solution)/shard_map/all_gather | solution.py:8
  57.8 4.3 %all-gather.1 = f32[16,32]{1,0:T(8,128)S(1)} all-gather(f32[8,32]{1,0:T(8,128)S(1)} %get-tuple-element.384), channel_id=3, replica_groups=mesh['gx'=4,'gy'=2,'gz'=4] {'gy'}, dimensions={0}, use_global_device_ids=true | all-gather | bytes 3072 | tf_op jit(solution)/shard_map/all_gather | solution.py:8
  62.2 5.2 %all_gather.47 = f32[4,8,32]{2,1,0:T(8,128)S(1)} all-gather(f32[1,8,32]{2,1,0:T(8,128)S(1)} %get-tuple-element.432), channel_id=1, replica_groups=mesh['gx'=4,'gy'=2,'gz'=4] {'gx'}, dimensions={0}, use_global_device_ids=true | all-gather | bytes 5120 | tf_op jit(solution)/shard_map/all_gather | solution.py:8
  67.3 5.2 %all_gather.44 = f32[4,8,32]{2,1,0:T(8,128)S(1)} all-gather(f32[1,8,32]{2,1,0:T(8,128)S(1)} %get-tuple-element.433), channel_id=1, replica_groups=mesh['gx'=4,'gy'=2,'gz'=4] {'gx'}, dimensions={0}, use_global_device_ids=true | all-gather | bytes 5120 | tf_op jit(solution)/shard_map/all_gather | solution.py:8
  72.5 6.4 %all-gather.2 = f32[16,32,128]{2,1,0:T(8,128)S(1)} all-gather(f32[8,32,128]{2,1,0:T(8,128)S(1)} %get-tuple-element.385), channel_id=4, replica_groups=mesh['gx'=4,'gy'=2,'gz'=4] {'gy'}, dimensions={0}, use_global_device_ids=true | all-gather | bytes 393216 | tf_op jit(solution)/shard_map/all_gather | solution.py:8
  79.0 7.2 %all_gather.50 = f32[4,8,32,128]{3,2,1,0:T(8,128)S(1)} all-gather(f32[1,8,32,128]{3,2,1,0:T(8,128)S(1)} %fusion.15), channel_id=1, replica_groups=mesh['gx'=4,'gy'=2,'gz'=4] {'gx'}, dimensions={0}, use_global_device_ids=true | all-gather | bytes 655360 | tf_op jit(solution)/shard_map/all_gather | solution.py:8
  86.2 0.6 while.46
  86.3 0.2 fusion.36
  86.5 0.2 fusion.36
  86.7 0.2 fusion.36
  86.9 0.2 multiply_reduce_fusion
  87.1 0.8 multiply_multiply_fusion
  87.9 0.6 log_add_fusion
  (25 shorter events, 0.7 us)
Async XLA Ops:
  0.6 0.8 copy-start
  24.2 62.9 %copy-start.2 = (f32[32,128]{1,0:T(8,128)S(1)}, f32[32,128]{1,0:T(8,128)}, u32[]{:S(2)}) copy-start(f32[32,128]{1,0:T(8,128)} %param.11) | copy-start | bytes 49156
  86.9 1.6 %copy-start.1 = (f32[8,32]{1,0:T(8,128)}, f32[8,32]{1,0:T(8,128)S(1)}, u32[]{:S(2)}) copy-start(f32[8,32]{1,0:T(8,128)S(1)} %get-tuple-element.382) | copy-start | bytes 3076
where the time goes:
time: 88.8 us; the launch traced here: 88.5 us
  blocking collectives  75.8 us (85%)
  matrix products  7.45 us (8%)
  other arithmetic  3.1 us (3%)
  local copies, waits for them, and re-layouts  1.28 us (1%)
    all_gather x9, blocking collectives, combined_all(): gathered = jax.tree.map(lambda a: lax.all_gather(a, axis), part)  75.8 us
    dot_general x1, matrix products, on_device(): jnp.einsum('bkgt,btkd->bkgd', weights, v_cache, preferred_element_type=jn...  4 us
    dot_general x1, matrix products, on_device(): jnp.einsum('bkgd,btkd->bkgt', grouped, k_cache, preferred_element_type=jn...  3.45 us

commit v1 on v0

--- a/solution.py
+++ b/solution.py
@@ -1,7 +1,17 @@
+import functools
+import math
+
 import jax
 import jax.numpy as jnp
 from jax import lax
+from jax.experimental import pallas as pl
+from jax.experimental.pallas import tpu as pltpu
 from jax.sharding import PartitionSpec as P
+
+AXES = ("gx", "gy", "gz")
+ROWS = 8
+LANES = 128
+MESH = pl.DeviceIdType.MESH
 
 
 def combined_all(part, axis, combine):
@@ -32,7 +42,7 @@
     return (highest, total, summed)
 
 
-def on_device(query, k_cache, v_cache, head_gain):
+def gathered_form(query, k_cache, v_cache, head_gain):
     batch_count, head_count, head_size = query.shape
     kv_count = k_cache.shape[2]
     group_size = head_count // kv_count
@@ -53,21 +63,237 @@
         precision=lax.Precision.HIGHEST,
     ).reshape(batch_count, head_count, head_size)
     local_peak = local_peak.reshape(batch_count, head_count)
-    partial_value = combined_all((local_peak, local_total, local_summed), "gz", pair_fold)
-    partial_value = combined_all(partial_value, "gy", pair_fold)
-    highest, total, summed = combined_all(partial_value, "gx", pair_fold)
+    partial_value = (local_peak, local_total, local_summed)
+    for axis in reversed(AXES):
+        partial_value = combined_all(partial_value, axis, pair_fold)
+    highest, total, summed = partial_value
     attended, log_norm = finish(summed, total, highest, head_gain[None, :, :])
     return (attended, log_norm, highest)
 
 
+def local_part(q_rows, keys, values, kv_count, scaling):
+    head_count = q_rows.shape[0]
+    columns = keys.shape[0]
+    group = head_count // kv_count
+    raw = lax.dot_general(
+        q_rows, keys, (((1,), (1,)), ((), ())), preferred_element_type=jnp.float32
+    )
+    head_of_row = lax.broadcasted_iota(jnp.int32, (head_count, LANES), 0) // group
+    kv_of_lane = lax.broadcasted_iota(jnp.int32, (head_count, LANES), 1) % kv_count
+    own = head_of_row == kv_of_lane
+    pieces = [
+        jnp.where(own, raw[:, c : c + LANES], -jnp.inf) for c in range(0, columns, LANES)
+    ]
+    peak = jnp.max(functools.reduce(jnp.maximum, pieces), axis=1, keepdims=True)
+    factor = scaling * math.log2(math.e)
+    high, low, running = [], [], None
+    for piece in pieces:
+        weight = jnp.exp2((piece - peak) * factor)
+        running = weight if running is None else running + weight
+        top = weight.astype(jnp.bfloat16)
+        high.append(top)
+        low.append((weight - top.astype(jnp.float32)).astype(jnp.bfloat16))
+    total = jnp.sum(running, axis=1, keepdims=True)
+    stacked = jnp.concatenate(
+        [jnp.concatenate(high, axis=1), jnp.concatenate(low, axis=1)], axis=0
+    )
+    both = jnp.dot(stacked, values, preferred_element_type=jnp.float32)
+    return peak * scaling, total, both[:head_count] + both[head_count:]
+
+
+def fused_kernel(
+    sizes, batch_count, kv_count, held_back,
+    q_ref, k_hbm, v_hbm, gain_ref,
+    out_ref, norm_ref, peak_ref,
+    k_buf, v_buf, part, part_stat, got, got_stat, fin_stat,
+    k_sem, v_sem, send_sem, recv_sem,
+):
+    size_x, size_y, size_z = sizes
+    count = size_x * size_y * size_z
+    head_count, head_size = gain_ref.shape
+    scaling = head_size ** (-0.5)
+    blocks = head_count // ROWS
+    me = (lax.axis_index("gx") * size_y + lax.axis_index("gy")) * size_z + lax.axis_index("gz")
+
+    def place(index):
+        return (index // (size_y * size_z), (index // size_z) % size_y, index % size_z)
+
+    own_batch = me // blocks
+    own_block = me % blocks
+    order = [(own_batch + 1 + i) % batch_count for i in range(batch_count)]
+
+    def loads(i):
+        return (
+            pltpu.make_async_copy(k_hbm.at[order[i]], k_buf.at[i], k_sem.at[i]),
+            pltpu.make_async_copy(v_hbm.at[order[i]], v_buf.at[i], v_sem.at[i]),
+        )
+
+    for i in range(batch_count):
+        for copy in loads(i):
+            copy.start()
+
+    barrier = pltpu.get_barrier_semaphore()
+
+    @pl.loop(1, count)
+    def _(step):
+        pl.semaphore_signal(
+            barrier, inc=1, device_id=place((me + step) % count), device_id_type=MESH
+        )
+
+    def send_part(owner):
+        slot = (me - owner + count) % count
+        for which, (src, dst) in enumerate(((part, got), (part_stat, got_stat))):
+            pltpu.make_async_remote_copy(
+                src_ref=src.at[owner],
+                dst_ref=dst.at[slot],
+                send_sem=send_sem.at[which],
+                recv_sem=recv_sem.at[which],
+                device_id=place(owner),
+                device_id_type=MESH,
+            ).start()
+
+    row = lax.broadcasted_iota(jnp.int32, (ROWS, LANES), 0)
+    lane = lax.broadcasted_iota(jnp.int32, (ROWS, LANES), 1)
+
+    def as_lanes(first, second, first_lane, second_lane):
+        spread = jnp.where(lane == row + first_lane, first, 0.0) + jnp.where(
+            lane == row + second_lane, second, 0.0
+        )
+        return jnp.sum(spread, axis=0, keepdims=True)
+
+    for i in range(batch_count):
+        batch = order[i]
+        for copy in loads(i):
+            copy.wait()
+        peak, total, summed = local_part(
+            q_ref[batch], k_buf[i], v_buf[i], kv_count, scaling
+        )
+        for g in range(blocks):
+            rows = slice(g * ROWS, (g + 1) * ROWS)
+            part[batch * blocks + g] = summed[rows]
+            part_stat[batch * blocks + g] = as_lanes(peak[rows], total[rows], 0, ROWS)
+        if i == held_back:
+            pl.semaphore_wait(barrier, count - 1)
+        if i >= held_back and i < batch_count - 1:
+            ready = range(i + 1) if i == held_back else (i,)
+            for j in ready:
+                for g in range(blocks):
+                    send_part(order[j] * blocks + g)
+    for step in range(1, blocks):
+        send_part(own_batch * blocks + (own_block + step) % blocks)
+    got[0] = part[me]
+    got_stat[0] = part_stat[me]
+
+    def wait_all(ref, sem):
+        span = ref.at[pl.ds(1, count - 1)]
+        pltpu.make_async_copy(span, span, sem).wait()
+
+    wait_all(got_stat, recv_sem.at[1])
+    stats = got_stat[...].reshape(count, LANES).T
+    peaks, totals = stats[:ROWS], stats[ROWS : 2 * ROWS]
+    highest = jnp.max(peaks, axis=1, keepdims=True)
+    factors = jnp.exp(peaks - highest)
+    total = jnp.sum(totals * factors, axis=1, keepdims=True)
+    wait_all(got, recv_sem.at[0])
+    terms = [got[s] * factors[:, s : s + 1] for s in range(count)]
+    while len(terms) > 1:
+        terms = [sum(terms[t : t + 2]) for t in range(0, len(terms), 2)]
+    gain_rows = gain_ref[pl.ds(pl.multiple_of(own_block * ROWS, ROWS), ROWS), :]
+    mixed = terms[0] / total
+    spread_sq = jnp.mean(mixed * mixed, axis=1, keepdims=True)
+    out_ref[me] = mixed * lax.rsqrt(spread_sq + 1e-06) * gain_rows
+    first = own_block * ROWS
+    fin_stat[me] = as_lanes(highest + jnp.log(total), highest, first, head_count + first)
+
+    @pl.loop(1, count)
+    def _(step):
+        peer = place((me + step) % count)
+        for which, ref in ((2, out_ref), (3, fin_stat)):
+            pltpu.make_async_remote_copy(
+                src_ref=ref.at[me],
+                dst_ref=ref.at[me],
+                send_sem=send_sem.at[which],
+                recv_sem=recv_sem.at[which],
+                device_id=peer,
+                device_id_type=MESH,
+            ).start()
+
+    for which, ref in enumerate((part, part_stat, out_ref, fin_stat)):
+        wait_all(ref, send_sem.at[which])
+    wait_all(fin_stat, recv_sem.at[3])
+    for b in range(batch_count):
+        line = fin_stat[b * blocks]
+        for g in range(1, blocks):
+            line = line + fin_stat[b * blocks + g]
+        norm_ref[b : b + 1, :] = line[:, :head_count]
+        peak_ref[b : b + 1, :] = line[:, head_count : 2 * head_count]
+    wait_all(out_ref, recv_sem.at[2])
+
+
+def fused_form(sizes, query, k_cache, v_cache, head_gain):
+    batch_count, head_count, head_size = query.shape
+    _, span, kv_count, _ = k_cache.shape
+    count = math.prod(sizes)
+    columns = span * kv_count
+    keys = k_cache.reshape(batch_count, columns, head_size)
+    values = v_cache.reshape(batch_count, columns, head_size)
+    vmem = pl.BlockSpec(memory_space=pltpu.VMEM)
+    hbm = pl.BlockSpec(memory_space=pl.ANY)
+    block = (count, ROWS, head_size)
+    line = (count, 1, LANES)
+    attended, log_norm, highest = pl.pallas_call(
+        functools.partial(fused_kernel, sizes, batch_count, kv_count, 3),
+        out_shape=(
+            jax.ShapeDtypeStruct(block, jnp.float32),
+            jax.ShapeDtypeStruct((batch_count, head_count), jnp.float32),
+            jax.ShapeDtypeStruct((batch_count, head_count), jnp.float32),
+        ),
+        in_specs=[vmem, hbm, hbm, vmem],
+        out_specs=(vmem, vmem, vmem),
+        scratch_shapes=[
+            pltpu.VMEM((batch_count, columns, head_size), k_cache.dtype),
+            pltpu.VMEM((batch_count, columns, head_size), v_cache.dtype),
+            pltpu.VMEM(block, jnp.float32),
+            pltpu.VMEM(line, jnp.float32),
+            pltpu.VMEM(block, jnp.float32),
+            pltpu.VMEM(line, jnp.float32),
+            pltpu.VMEM(line, jnp.float32),
+            pltpu.SemaphoreType.DMA((batch_count,)),
+            pltpu.SemaphoreType.DMA((batch_count,)),
+            pltpu.SemaphoreType.DMA((4,)),
+            pltpu.SemaphoreType.DMA((4,)),
+        ],
+        compiler_params=pltpu.CompilerParams(
+            collective_id=0, has_side_effects=True, vmem_limit_bytes=48 * 1024 * 1024
+        ),
+    )(query, keys, values, head_gain)
+    return attended.reshape(query.shape), log_norm, highest
+
+
+def on_device(sizes, query, k_cache, v_cache, head_gain):
+    batch_count, head_count, head_size = query.shape
+    columns = k_cache.shape[1] * k_cache.shape[2]
+    count = math.prod(sizes)
+    fits = (
+        batch_count * head_count == count * ROWS
+        and head_count % ROWS == 0
+        and 2 * head_count <= LANES
+        and head_size == LANES
+        and columns % LANES == 0
+        and LANES % k_cache.shape[2] == 0
+    )
+    if fits:
+        return fused_form(sizes, query, k_cache, v_cache, head_gain)
+    return gathered_form(query, k_cache, v_cache, head_gain)
+
+
 def solution(mesh):
-    in_specs = (
-        P(),
-        P(None, ("gx", "gy", "gz"), None, None),
-        P(None, ("gx", "gy", "gz"), None, None),
-        P(),
-    )
-    out_specs = (P(), P(), P())
+    sizes = tuple(mesh.shape[a] for a in AXES)
+    in_specs = (P(), P(None, AXES, None, None), P(None, AXES, None, None), P())
     return jax.shard_map(
-        on_device, mesh=mesh, in_specs=in_specs, out_specs=out_specs, check_vma=False
-    )
+        functools.partial(on_device, sizes),
+        mesh=mesh,
+        in_specs=in_specs,
+        out_specs=(P(), P(), P()),
+        check_vma=False,
+    )

time: 88.8 us -> 26.8 us (0.30)
  blocking collectives: 75.8 us -> 0 us
  Pallas kernels: 0 us -> 20.4 us
  matrix products: 7.45 us -> 0 us
  local copies, waits for them, and re-layouts: 1.28 us -> 5.58 us
  other arithmetic: 3.1 us -> 0 us
    all_gather x9 -> x0, blocking collectives: 75.8 us -> none  [combined_all(): gathered = jax.tree.map(lambda a: lax.all_gather(a, axis), part)]
    pallas_call x0 -> x1, Pallas kernels: none -> 20.4 us  [fused_form(): pl.pallas_call(functools.partial(fused_kernel, sizes, batch_count, kv_cou...]
    dot_general x2 -> x0, matrix products: 7.45 us -> none  [the longest x1 4 us: on_device(): jnp.einsum('bkgt,btkd->bkgd', weights, v_cache, preferred_element_type=jn...]
    unnamed x6 -> x9, local copies, waits for them, and re-layouts: 0.85 us -> 5.58 us
    add x15 -> x0, other arithmetic: 1.84 us -> none  [the longest x7 1.13 us: pair_fold(): summed_one * scale_one[..., None] + summed_two * scale_two[..., None]]
where the time goes in v1:
time: 26.8 us; the launch traced here: 26.6 us
  Pallas kernels  20.4 us (76%)
  local copies, waits for them, and re-layouts  5.58 us (21%)
  between operations  0.65 us (2%)
    pallas_call x1, Pallas kernels, fused_form(): pl.pallas_call(functools.partial(fused_kernel, sizes, batch_count, kv_cou...  20.4 us
    unnamed x9, local copies, waits for them, and re-layouts  5.58 us

profile of v1, /device:TPU:0, one launch (start us, length us, event | category | flops | bytes accessed | tf_op | source)
XLA Modules:
  0.0 26.6 jit_solution(8915535150557604142)
XLA Ops:
  0.6 0.0 copy-start
  0.6 2.2 %copy-done = bf16[8,256,8,128]{3,2,1,0:T(8,128)(2,1)S(1)} copy-done((bf16[8,256,8,128]{3,2,1,0:T(8,128)(2,1)S(1)}, bf16[8,256,8,128]{3,2,1,0:T(8,128)(2,1)}, u32[]{:S(2)}) %copy-start) | copy-done | bytes 4194328
  2.8 0.0 copy-start.1
  2.8 0.8 %copy-done.1 = bf16[8,32,128]{2,1,0:T(8,128)(2,1)S(1)} copy-done((bf16[8,32,128]{2,1,0:T(8,128)(2,1)S(1)}, bf16[8,32,128]{2,1,0:T(8,128)(2,1)}, u32[]{:S(2)}) %copy-start.1) | copy-done | bytes 65560
  3.7 0.0 copy-start.2
  3.7 0.7 %copy-done.2 = f32[32,128]{1,0:T(8,128)S(1)} copy-done((f32[32,128]{1,0:T(8,128)S(1)}, f32[32,128]{1,0:T(8,128)}, u32[]{:S(2)}) %copy-start.2) | copy-done | bytes 16408
  4.4 20.4 %shard_map.67 = (f32[32,8,128]{2,1,0:T(8,128)S(1)}, f32[8,32]{1,0:T(8,128)S(1)}, f32[8,32]{1,0:T(8,128)S(1)}) custom-call(bf16[8,32,128]{2,1,0:T(8,128)(2,1)S(1)} %copy-done.1, bf16[8,2048,128]{2,1,0:T(8,128)(2,1)S(1)} %bitcast.3, bf16[8,2048,128]{2,1,0:T(8,128)(2,1)} %bitcast.5, f32[32,128]{1,0:T(8,128)S(1)} %copy-done.2), custom_call_target="tpu_custom_call" | custom-call | tf_op jit(solution)/shard_map/pallas_call | solution.py:244
  24.7 0.7 %copy.10 = f32[8,32,128]{2,1,0:T(8,128)} copy(f32[8,32,128]{2,1,0:T(8,128)S(1)} %bitcast.4) | data formatting | bytes 262144
  25.4 0.6 %copy.11 = f32[8,32]{1,0:T(8,128)} copy(f32[8,32]{1,0:T(8,128)S(1)} %get-tuple-element.13) | data formatting | bytes 2048
  26.0 0.6 %copy.12 = f32[8,32]{1,0:T(8,128)} copy(f32[8,32]{1,0:T(8,128)S(1)} %get-tuple-element.14) | data formatting | bytes 2048
Async XLA Ops:
  0.6 2.2 %copy-start = (bf16[8,256,8,128]{3,2,1,0:T(8,128)(2,1)S(1)}, bf16[8,256,8,128]{3,2,1,0:T(8,128)(2,1)}, u32[]{:S(2)}) copy-start(bf16[8,256,8,128]{3,2,1,0:T(8,128)(2,1)} %param.5) | copy-start | bytes 12582916
  2.8 0.8 %copy-start.1 = (bf16[8,32,128]{2,1,0:T(8,128)(2,1)S(1)}, bf16[8,32,128]{2,1,0:T(8,128)(2,1)}, u32[]{:S(2)}) copy-start(bf16[8,32,128]{2,1,0:T(8,128)(2,1)} %q_ref.1) | copy-start | bytes 196612
  3.7 0.7 %copy-start.2 = (f32[32,128]{1,0:T(8,128)S(1)}, f32[32,128]{1,0:T(8,128)}, u32[]{:S(2)}) copy-start(f32[32,128]{1,0:T(8,128)} %gain_ref.1) | copy-start | bytes 49156

commit v2 on v1

--- a/solution.py
+++ b/solution.py
@@ -103,10 +103,10 @@
 
 def fused_kernel(
     sizes, batch_count, kv_count, held_back,
-    q_ref, k_hbm, v_hbm, gain_ref,
+    q_hbm, k_hbm, v_hbm, gain_hbm,
     out_ref, norm_ref, peak_ref,
-    k_buf, v_buf, part, part_stat, got, got_stat, fin_stat,
-    k_sem, v_sem, send_sem, recv_sem,
+    q_ref, gain_ref, k_buf, v_buf, part, part_stat, got, got_stat, fin_stat,
+    side_sem, k_sem, v_sem, send_sem, recv_sem,
 ):
     size_x, size_y, size_z = sizes
     count = size_x * size_y * size_z
@@ -128,9 +128,13 @@
             pltpu.make_async_copy(v_hbm.at[order[i]], v_buf.at[i], v_sem.at[i]),
         )
 
+    q_load = pltpu.make_async_copy(q_hbm, q_ref, side_sem.at[0])
+    gain_load = pltpu.make_async_copy(gain_hbm, gain_ref, side_sem.at[1])
+    q_load.start()
     for i in range(batch_count):
         for copy in loads(i):
             copy.start()
+    gain_load.start()
 
     barrier = pltpu.get_barrier_semaphore()
 
@@ -161,6 +165,7 @@
         )
         return jnp.sum(spread, axis=0, keepdims=True)
 
+    q_load.wait()
     for i in range(batch_count):
         batch = order[i]
         for copy in loads(i):
@@ -198,6 +203,7 @@
     terms = [got[s] * factors[:, s : s + 1] for s in range(count)]
     while len(terms) > 1:
         terms = [sum(terms[t : t + 2]) for t in range(0, len(terms), 2)]
+    gain_load.wait()
     gain_rows = gain_ref[pl.ds(pl.multiple_of(own_block * ROWS, ROWS), ROWS), :]
     mixed = terms[0] / total
     spread_sq = jnp.mean(mixed * mixed, axis=1, keepdims=True)
@@ -238,7 +244,7 @@
     keys = k_cache.reshape(batch_count, columns, head_size)
     values = v_cache.reshape(batch_count, columns, head_size)
     vmem = pl.BlockSpec(memory_space=pltpu.VMEM)
-    hbm = pl.BlockSpec(memory_space=pl.ANY)
+    hbm = pl.BlockSpec(memory_space=pltpu.HBM)
     block = (count, ROWS, head_size)
     line = (count, 1, LANES)
     attended, log_norm, highest = pl.pallas_call(
@@ -248,9 +254,11 @@
             jax.ShapeDtypeStruct((batch_count, head_count), jnp.float32),
             jax.ShapeDtypeStruct((batch_count, head_count), jnp.float32),
         ),
-        in_specs=[vmem, hbm, hbm, vmem],
+        in_specs=[hbm] * 4,
         out_specs=(vmem, vmem, vmem),
         scratch_shapes=[
+            pltpu.VMEM(query.shape, query.dtype),
+            pltpu.VMEM(head_gain.shape, head_gain.dtype),
             pltpu.VMEM((batch_count, columns, head_size), k_cache.dtype),
             pltpu.VMEM((batch_count, columns, head_size), v_cache.dtype),
             pltpu.VMEM(block, jnp.float32),
@@ -258,13 +266,14 @@
             pltpu.VMEM(block, jnp.float32),
             pltpu.VMEM(line, jnp.float32),
             pltpu.VMEM(line, jnp.float32),
+            pltpu.SemaphoreType.DMA((2,)),
             pltpu.SemaphoreType.DMA((batch_count,)),
             pltpu.SemaphoreType.DMA((batch_count,)),
             pltpu.SemaphoreType.DMA((4,)),
             pltpu.SemaphoreType.DMA((4,)),
         ],
         compiler_params=pltpu.CompilerParams(
-            collective_id=0, has_side_effects=True, vmem_limit_bytes=48 * 1024 * 1024
+            collective_id=0, has_side_effects=True, vmem_limit_bytes=61 * 1024 * 1024
         ),
     )(query, keys, values, head_gain)
     return attended.reshape(query.shape), log_norm, highest

time: 26.8 us -> 27.1 us (1.011)
  Pallas kernels: 20.4 us -> 22.1 us
  local copies, waits for them, and re-layouts: 5.58 us -> 4.11 us
    pallas_call x1, Pallas kernels: 20.4 us -> 22.1 us  [fused_form(): pl.pallas_call(functools.partial(fused_kernel, sizes, batch_count, kv_cou...]
    unnamed x9 -> x3, local copies, waits for them, and re-layouts: 5.58 us -> 4.11 us
where the time goes in v2:
time: 27.1 us; the launch traced here: 26.8 us
  Pallas kernels  22.1 us (82%)
  local copies, waits for them, and re-layouts  4.11 us (15%)
  between operations  0.64 us (2%)
    pallas_call x1, Pallas kernels, fused_form(): pl.pallas_call(functools.partial(fused_kernel, sizes, batch_count, kv_cou...  22.1 us
    unnamed x3, local copies, waits for them, and re-layouts  4.11 us

profile of v2, /device:TPU:0, one launch (start us, length us, event | category | flops | bytes accessed | tf_op | source)
XLA Modules:
  0.0 26.8 jit_solution(999167985359151490)
XLA Ops:
  0.6 22.1 %shard_map.67 = (f32[32,8,128]{2,1,0:T(8,128)}, f32[8,32]{1,0:T(8,128)}, f32[8,32]{1,0:T(8,128)}) custom-call(bf16[8,32,128]{2,1,0:T(8,128)(2,1)} %q_hbm.1, bf16[8,2048,128]{2,1,0:T(8,128)(2,1)} %bitcast.3, bf16[8,2048,128]{2,1,0:T(8,128)(2,1)} %bitcast.4, f32[32,128]{1,0:T(8,128)} %gain_hbm.1), custom_call_target="tpu_custom_call" | custom-call | tf_op jit(solution)/shard_map/pallas_call | solution.py:250
  22.7 1.6 %copy.10 = f32[8,32,128]{2,1,0:T(8,128)} copy(f32[8,32,128]{2,1,0:T(8,128)} %bitcast.5) | data formatting | bytes 262144
  24.3 1.3 %copy.11 = f32[8,32]{1,0:T(8,128)} copy(f32[8,32]{1,0:T(8,128)} %get-tuple-element.13) | data formatting | bytes 2048
  25.6 1.3 %copy.12 = f32[8,32]{1,0:T(8,128)} copy(f32[8,32]{1,0:T(8,128)} %get-tuple-element.14) | data formatting | bytes 2048

commit v3 on v2

--- a/solution.py
+++ b/solution.py
@@ -273,9 +273,9 @@
             pltpu.SemaphoreType.DMA((4,)),
         ],
         compiler_params=pltpu.CompilerParams(
-            collective_id=0, has_side_effects=True, vmem_limit_bytes=61 * 1024 * 1024
+            collective_id=0, has_side_effects=True, vmem_limit_bytes=48 * 1024 * 1024
         ),
-    )(query, keys, values, head_gain)
+    )(*(pltpu.with_memory_space_constraint(a, pltpu.HBM) for a in (query, keys, values, head_gain)))
     return attended.reshape(query.shape), log_norm, highest
 
 

time: 27.1 us -> 24 us (0.89)
  local copies, waits for them, and re-layouts: 4.11 us -> 1.84 us
  Pallas kernels: 22.1 us -> 21.4 us
    unnamed x3, local copies, waits for them, and re-layouts: 4.11 us -> 1.84 us
    pallas_call x1, Pallas kernels: 22.1 us -> 21.4 us  [fused_form(): pl.pallas_call(functools.partial(fused_kernel, sizes, batch_count, kv_cou...]
where the time goes in v3:
time: 24 us; the launch traced here: 23.9 us
  Pallas kernels  21.4 us (89%)
  local copies, waits for them, and re-layouts  1.84 us (8%)
  between operations  0.64 us (3%)
    pallas_call x1, Pallas kernels, fused_form(): pl.pallas_call(functools.partial(fused_kernel, sizes, batch_count, kv_cou...  21.4 us
    unnamed x3, local copies, waits for them, and re-layouts  1.84 us

profile of v3, /device:TPU:0, one launch (start us, length us, event | category | flops | bytes accessed | tf_op | source)
XLA Modules:
  0.0 23.9 jit_solution(6708337647671361544)
XLA Ops:
  0.6 21.4 %shard_map.67 = (f32[32,8,128]{2,1,0:T(8,128)S(1)}, f32[8,32]{1,0:T(8,128)S(1)}, f32[8,32]{1,0:T(8,128)S(1)}) custom-call(bf16[8,32,128]{2,1,0:T(8,128)(2,1)} %q_hbm.1, bf16[8,2048,128]{2,1,0:T(8,128)(2,1)} %bitcast.4, bf16[8,2048,128]{2,1,0:T(8,128)(2,1)} %bitcast.5, f32[32,128]{1,0:T(8,128)} %gain_hbm.1), custom_call_target="tpu_custom_call" | custom-call | tf_op jit(solution)/shard_map/pallas_call | solution.py:250
  22.1 0.7 %copy.10 = f32[8,32,128]{2,1,0:T(8,128)} copy(f32[8,32,128]{2,1,0:T(8,128)S(1)} %bitcast.3) | data formatting | bytes 262144
  22.7 0.6 %copy.11 = f32[8,32]{1,0:T(8,128)} copy(f32[8,32]{1,0:T(8,128)S(1)} %get-tuple-element.13) | data formatting | bytes 2048
  23.3 0.6 %copy.12 = f32[8,32]{1,0:T(8,128)} copy(f32[8,32]{1,0:T(8,128)S(1)} %get-tuple-element.14) | data formatting | bytes 2048
